TPU v7x, 128 devices: a whole 4x4x4 slice. The times are simulated.
128 devices in a mesh: dp: 64 (over z, y, x), mp: 2 (over core).
Axes of the slice: x: 4, y: 4, z: 4, core: 2. Of those that a mesh axis runs over, the one named last changes fastest.
Arguments:
- hot_rows: int32 [64, 64, 32], P('dp'), may hold values from 0 to 4095
- hot_count: int32 [64, 64], P('dp'), may hold values from 1 to 32, as said below
- hot_cot: bfloat16 [64, 64, 32, 128], P('dp'), may hold values from -6 to 6
- table: float32 [262144, 128], P('dp'), may hold values from -3 to 3
- cold_ids: int32 [65536], P('dp'), may hold values from 0 to 1048575
- hash_mult: int32 [1024], replicated, may hold values from 1 to 1023
- hash_add: int32 [1024], replicated, may hold values from 0 to 1000002
- layer_one: bfloat16 [1024, 1024], P(None, 'mp'), may hold values from -0.1875 to 0.1875
- layer_two: bfloat16 [1024, 1024], P('mp'), may hold values from -0.1875 to 0.1875
- layer_three: bfloat16 [1024, 1024], P(None, 'mp'), may hold values from -0.1875 to 0.1875
- layer_four: bfloat16 [1024, 128], P('mp'), may hold values from -0.1875 to 0.1875
- cold_cot: bfloat16 [65536, 128], P('dp'), may hold values from -6 to 6
Outputs:
- hot_emb: bfloat16 [64, 64, 32, 128], P('dp')
- new_table: float32 [262144, 128], P('dp')
- cold_emb: bfloat16 [65536, 128], P('dp')
- grad_one: float32 [1024, 1024], P(None, 'mp')
- grad_two: float32 [1024, 1024], P('mp')
- grad_three: float32 [1024, 1024], P(None, 'mp')
- grad_four: float32 [1024, 128], P('mp')
Inputs may be any that keep to these rules, and one draw needn't show every extreme that they name: `hot_rows`: entries index the owner's block of 4096 rows; entries in unused slots are arbitrary. `hot_count`: every batch shard fills all 32 slots of some owner, and some owner receives 32 from every batch shard.
All inputs are finite; a program needn't handle non-finite values.
Results may differ from a plain program's by a relative error of at most 0.0074.
Values may be sent and summed in bfloat16 or wider, within the bound.
A program may use at most 128 MiB of HBM per device.

v0:
```python
import jax
import jax.numpy as jnp
from jax import lax
from jax.sharding import PartitionSpec as P

COLD = 1024
learn_rate = 0.5
modulus = 1000003


def over_pieces(array, axis):
    return lax.all_gather(array, axis).sum(0)


def from_everyone(array, axis):
    size = lax.axis_size(axis)
    return lax.all_to_all(
        jnp.broadcast_to(array[None], (size, *array.shape)), axis, 0, 0, tiled=True
    )


def over_copies(array, axis):
    everything = from_everyone(array, axis)
    return jnp.sum(everything, axis=0)


def in_order(tiles, dim):
    dims = list(tiles.shape[1:])
    dims[dim] *= tiles.shape[0]
    return jnp.moveaxis(tiles, 0, dim).reshape(dims)


def gather_directly(array, axis, dim):
    return in_order(from_everyone(array, axis), dim)


def features_of(ids, hash_mult, hash_add):
    hashed = jnp.remainder(ids[:, None] * hash_mult[None, :] + hash_add[None, :], modulus)
    return (hashed.astype(jnp.float32) * (2.0 / 1000002.0) - 1.0).astype(jnp.bfloat16)


def silu_grad(value):
    sig = jax.nn.sigmoid(value)
    return sig * (1.0 + value * (1.0 - sig))


def local(
    hot_rows,
    hot_count,
    hot_cot,
    table,
    cold_ids,
    hash_mult,
    hash_add,
    layer_one,
    layer_two,
    layer_three,
    layer_four,
    cold_cot,
):
    width = table.shape[1]
    slots_all = hot_rows.shape[2]
    span = slots_all // lax.axis_size("mp")
    begin = lax.axis_index("mp") * span
    mine = lax.dynamic_slice_in_dim(hot_rows, begin, span, 2)
    received = lax.all_to_all(mine, "dp", split_axis=1, concat_axis=1, tiled=True)
    fetched = jnp.take(table, received.reshape(-1), axis=0).astype(jnp.bfloat16)
    fetched = fetched.reshape(received.shape + (width,))
    returned = lax.all_to_all(fetched, "dp", split_axis=1, concat_axis=1, tiled=True)
    returned, received = (returned, received)
    feats = features_of(cold_ids, hash_mult, hash_add)
    pre_one = jnp.dot(feats, layer_one, preferred_element_type=jnp.float32)
    act_one = jax.nn.silu(pre_one).astype(jnp.bfloat16)
    pre_two = over_pieces(jnp.dot(act_one, layer_two, preferred_element_type=jnp.float32), "mp")
    act_two = jax.nn.silu(pre_two).astype(jnp.bfloat16)
    pre_three = jnp.dot(act_two, layer_three, preferred_element_type=jnp.float32)
    act_three = jax.nn.silu(pre_three).astype(jnp.bfloat16)
    cold_emb = over_copies(
        jnp.dot(act_three, layer_four, preferred_element_type=jnp.float32), "mp"
    ).astype(jnp.bfloat16)
    slot_index = begin + jnp.arange(span, dtype=jnp.int32)
    used = slot_index[None, None, :] < hot_count[:, :, None]
    own_emb = jnp.where(used[..., None], returned, jnp.zeros_like(returned))
    own_cot = lax.dynamic_slice_in_dim(hot_cot, begin, span, 2)
    own_cot = jnp.where(used[..., None], own_cot, jnp.zeros_like(own_cot))
    arrived = lax.all_to_all(own_cot, "dp", split_axis=1, concat_axis=1, tiled=True)
    factor = float(COLD * lax.axis_size("dp")) ** (-0.5)
    back_three = (
        jnp.dot(cold_cot, layer_four.T, preferred_element_type=jnp.float32) * silu_grad(pre_three)
    ).astype(jnp.bfloat16)
    part_four = jnp.dot(act_three.T, cold_cot, preferred_element_type=jnp.float32) * factor
    back_sum = over_pieces(
        jnp.dot(back_three, layer_three.T, preferred_element_type=jnp.float32), "mp"
    )
    part_three = jnp.dot(act_two.T, back_three, preferred_element_type=jnp.float32) * factor
    back_two = (back_sum * silu_grad(pre_two)).astype(jnp.bfloat16)
    part_two = jnp.dot(act_one.T, back_two, preferred_element_type=jnp.float32) * factor
    back_one = (
        jnp.dot(back_two, layer_two.T, preferred_element_type=jnp.float32) * silu_grad(pre_one)
    ).astype(jnp.bfloat16)
    part_one = jnp.dot(feats.T, back_one, preferred_element_type=jnp.float32) * factor
    part_one, part_two, part_three, part_four = lax.psum(
        (part_one, part_two, part_three, part_four), "dp"
    )
    arrived = gather_directly(arrived, "mp", 2)
    received = gather_directly(received, "mp", 2)
    hot_emb = gather_directly(own_emb, "mp", 2)
    delta = (
        jnp.zeros_like(table)
        .at[received.reshape(-1)]
        .add(arrived.reshape(-1, width).astype(jnp.float32))
    )
    new_table = table - learn_rate * delta
    return (hot_emb, new_table, cold_emb, part_one, part_two, part_three, part_four)


def solution(mesh):
    in_specs = (
        P("dp", None, None),
        P("dp", None),
        P("dp", None, None, None),
        P("dp", None),
        P("dp"),
        P(),
        P(),
        P(None, "mp"),
        P("mp", None),
        P(None, "mp"),
        P("mp", None),
        P("dp", None),
    )
    out_specs = (
        P("dp", None, None, None),
        P("dp", None),
        P("dp", None),
        P(None, "mp"),
        P("mp", None),
        P(None, "mp"),
        P("mp", None),
    )
    return jax.shard_map(local, mesh=mesh, in_specs=in_specs, out_specs=out_specs, check_vma=False)
```

profile of v0, /device:TPU:1, one launch (start us, length us, event | category | flops | bytes accessed | tf_op | source)
XLA Modules:
  0.0 269.9 jit_solution(9633521886486711486)
XLA Ops:
  7.2 4.8 %fusion.9 = f32[1024,512]{1,0:T(8,128)S(1)} fusion(bf16[1024,512]{1,0:T(8,128)(2,1)} %param.19, s32[1024]{0:T(1024)} %param.18, s32[1024]{0:T(1024)} %param.17, s32[1024]{0:T(1024)} %param.16), kind=kOutput, calls=%fused_computation.21 | convolution fusion | flops 1086324736 | bytes 3158016 | tf_op jit(solution)/shard_map/dot_general | solution.py:72
  12.0 1.3 copy-done.19
  13.4 3.3 %fusion.25 = f32[1024,1024]{1,0:T(8,128)} fusion(bf16[512,1024]{1,0:T(8,128)(2,1)S(1)} %copy-done.14, f32[1024,512]{1,0:T(8,128)S(1)} %fusion.9), kind=kOutput, calls=%fused_computation.50 | convolution fusion | flops 1076363264 | bytes 7340032 | tf_op jit(solution)/shard_map/dot_general | solution.py:74
  16.7 26.3 %all-gather.5.cloned.1.call-done = f32[2048,1024]{1,0:T(8,128)} async-done(((f32[1024,1024]{1,0:T(8,128)}), f32[2048,1024]{1,0:T(8,128)}) %all-gather.5.cloned.1.call-update) | async-done | bytes 8388624 | tf_op jit(solution)/shard_map/all_gather | solution.py:12
  43.0 6.7 %reduce_sum.27 = f32[1024,1024]{1,0:T(8,128)} reduce(f32[2,1024,1024]{2,1,0:T(8,128)} %bitcast.44, f32[]{:T(128)} %constant.31.clone.1), dimensions={0}, to_apply=%region_1.2 | reduce | flops 1048576 | bytes 12582916 | tf_op jit(solution)/shard_map/reduce_sum | solution.py:12
  49.6 3.3 %multiply_convert_fusion.1 = bf16[1024,1024]{1,0:T(8,128)(2,1)S(1)} fusion(f32[1024,1024]{1,0:T(8,128)} %reduce_sum.27), kind=kLoop, calls=%fused_computation.8 | loop fusion | flops 5242880 | bytes 6291456 | tf_op jit(solution)/shard_map/convert_element_type | solution.py:75
  53.0 1.5 multiply_convert_fusion.4
  54.6 0.9 multiply_convert_fusion.3
  55.4 3.2 %fusion.27 = f32[1024,1024]{1,0:T(8,128)} fusion(bf16[1024,512]{1,0:T(8,128)(2,1)S(1)} %multiply_convert_fusion.3, bf16[1024,512]{1,0:T(8,128)(2,1)S(1)} %copy-done), kind=kOutput, calls=%fused_computation.54 | convolution fusion | flops 1073741824 | bytes 6291456 | tf_op jit(solution)/shard_map/dot_general | solution.py:93
  58.9 1.2 convolution_multiply_fusion.2
  60.1 4.2 %convolution_multiply_fusion = f32[1024,512]{1,0:T(8,128)} fusion(bf16[1024,1024]{1,0:T(8,128)(2,1)} %copy-done.5, bf16[1024,512]{1,0:T(8,128)(2,1)S(1)} %multiply_convert_fusion.3), kind=kOutput, calls=%fused_computation.23 | convolution fusion | flops 1074266112 | bytes 5242880 | tf_op jit(solution)/shard_map/dot_general | solution.py:95
  64.3 18.4 %all-gather.7.cloned.1.call-done = f32[2048,1024]{1,0:T(8,128)} async-done(((f32[1024,1024]{1,0:T(8,128)}), f32[2048,1024]{1,0:T(8,128)}) %all-gather.7.cloned.1.call-update) | async-done | bytes 8388624 | tf_op jit(solution)/shard_map/all_gather | solution.py:12
  82.8 6.6 %reduce_sum.29 = f32[1024,1024]{1,0:T(8,128)} reduce(f32[2,1024,1024]{2,1,0:T(8,128)} %bitcast.43, f32[]{:T(128)} %constant.31.clone.1), dimensions={0}, to_apply=%region_3.4 | reduce | flops 1048576 | bytes 12582916 | tf_op jit(solution)/shard_map/reduce_sum | solution.py:12
  89.4 5.0 %multiply_convert_fusion = bf16[1024,1024]{1,0:T(8,128)(2,1)S(1)} fusion(f32[1024,1024]{1,0:T(8,128)} %reduce_sum.29, f32[1024,1024]{1,0:T(8,128)} %reduce_sum.27), kind=kLoop, calls=%fused_computation.7 | loop fusion | flops 9437184 | bytes 10485760 | tf_op jit(solution)/shard_map/convert_element_type | solution.py:96
  94.5 2.6 convolution_multiply_fusion.1
  97.2 8.1 %fusion.11 = f32[1024,512]{1,0:T(8,128)} fusion(s32[1024]{0:T(1024)S(1)} %copy-done.16, s32[1024]{0:T(1024)S(1)} %copy-done.17, s32[1024]{0:T(1024)S(1)} %copy-done.18, f32[1024,512]{1,0:T(8,128)} %copy-done.19, bf16[1024,1024]{1,0:T(8,128)(2,1)S(1)} %multiply_convert_fusion, bf16[512,1024]{1,0:T(8,128)(2,1)S(1)} %copy-done.15), kind=kOutput, calls=%fused_computation.25 | convolution fusion | flops 2165309440 | bytes 7352320 | tf_op jit(solution)/shard_map/dot_general | solution.py:101
  105.4 0.7 copy-done.12
  106.0 0.7 copy.43
  106.7 10.1 %all-to-all-start = ((s32[1,64,16]{2,0,1:T(1,128)}), s32[1,64,16]{2,0,1:T(1,128)S(1)}, u32[]{:S(2)}, u32[]{:S(2)}) async-start(s32[1,64,16]{2,0,1:T(1,128)} %copy.43), calls=%async_computation | async-start | bytes 65536 | tf_op jit(solution)/shard_map/all_to_all | solution.py:66
  116.8 8.7 %all-to-all-done = s32[1,64,16]{2,0,1:T(1,128)S(1)} async-done(((s32[1,64,16]{2,0,1:T(1,128)}), s32[1,64,16]{2,0,1:T(1,128)S(1)}, u32[]{:S(2)}, u32[]{:S(2)}) %all-to-all-start) | async-done | bytes 4128 | tf_op jit(solution)/shard_map/all_to_all | solution.py:66
  125.6 0.7 reshape.200
  126.3 4.9 %all-to-all-start.3 = ((s32[2,1,1024]{2,1,0:T(1,128)}), s32[2,1,1024]{2,1,0:T(1,128)S(1)}, u32[]{:S(2)}, u32[]{:S(2)}) async-start(s32[2,1,1024]{2,1,0:T(1,128)} %reshape.200), calls=%async_computation.3 | async-start | bytes 16384 | tf_op jit(solution)/shard_map/all_to_all | solution.py:17
  131.1 0.5 broadcast.139
  131.7 0.7 reduce.3
  132.5 2.9 %gather_fusion = bf16[1024,128]{1,0:T(8,128)(2,1)S(1)} fusion(f32[4096,128]{1,0:T(8,128)S(1)} %copy-done.2, s32[1024]{0:T(1024)S(1)} %broadcast_clamp_fusion), kind=kCustom, calls=%fused_computation | custom fusion | bytes 528384 | tf_op jit(solution)/shard_map/jit(_take)/gather | solution.py:67
  135.4 0.9 select_convert_fusion
  136.3 4.6 %all-to-all-start.1 = ((bf16[1,64,16,128]{3,2,0,1:T(8,128)(2,1)}), bf16[1,64,16,128]{3,2,0,1:T(8,128)(2,1)S(1)}, u32[]{:S(2)}, u32[]{:S(2)}) async-start(bf16[1,64,16,128]{3,2,0,1:T(8,128)(2,1)} %select_convert_fusion), calls=%async_computation.1 | async-start | bytes 524288 | tf_op jit(solution)/shard_map/all_to_all | solution.py:69
  141.1 0.5 broadcast.140
  141.6 0.7 reduce.4
  142.6 8.5 %all-to-all-done.1 = bf16[1,64,16,128]{3,2,0,1:T(8,128)(2,1)S(1)} async-done(((bf16[1,64,16,128]{3,2,0,1:T(8,128)(2,1)}), bf16[1,64,16,128]{3,2,0,1:T(8,128)(2,1)S(1)}, u32[]{:S(2)}, u32[]{:S(2)}) %all-to-all-start.1) | async-done | bytes 262176 | tf_op jit(solution)/shard_map/all_to_all | solution.py:69
  151.1 0.9 dynamic-slice_select_fusion
  152.1 5.2 %all_to_all.35 = bf16[2,1,64,16,128]{4,3,2,1,0:T(8,128)(2,1)S(1)} all-to-all(bf16[2,1,64,16,128]{4,3,2,1,0:T(8,128)(2,1)S(1)} %broadcast_in_dim.64), channel_id=1, replica_groups=mesh['dp'=64,'mp'=2] {'mp'}, dimensions={0} | all-to-all | bytes 1048576 | tf_op jit(solution)/shard_map/all_to_all | solution.py:17
  157.3 4.6 %all-to-all-start.4 = ((bf16[1,64,16,128]{3,2,0,1:T(8,128)(2,1)}), bf16[1,64,16,128]{3,2,0,1:T(8,128)(2,1)S(1)}, u32[]{:S(2)}, u32[]{:S(2)}) async-start(bf16[1,64,16,128]{3,2,0,1:T(8,128)(2,1)} %get-tuple-element.11), calls=%async_computation.4 | async-start | bytes 524288 | tf_op jit(solution)/shard_map/all_to_all | solution.py:86
  162.0 0.8 copy.38
  162.8 9.2 %all-to-all-done.4 = bf16[1,64,16,128]{3,2,0,1:T(8,128)(2,1)S(1)} async-done(((bf16[1,64,16,128]{3,2,0,1:T(8,128)(2,1)}), bf16[1,64,16,128]{3,2,0,1:T(8,128)(2,1)S(1)}, u32[]{:S(2)}, u32[]{:S(2)}) %all-to-all-start.4) | async-done | bytes 262176 | tf_op jit(solution)/shard_map/all_to_all | solution.py:86
  172.1 5.3 %all_to_all.36 = bf16[2,1,64,16,128]{4,3,2,1,0:T(8,128)(2,1)S(1)} all-to-all(bf16[2,1,64,16,128]{4,3,2,1,0:T(8,128)(2,1)S(1)} %broadcast_in_dim.68), channel_id=1, replica_groups=mesh['dp'=64,'mp'=2] {'mp'}, dimensions={0} | all-to-all | bytes 1048576 | tf_op jit(solution)/shard_map/all_to_all | solution.py:17
  177.3 1.1 copy_convert_fusion
  178.5 13.2 %scatter_custom_fusion = f32[4096,128]{1,0:T(8,128)} fusion(s32[2048]{0:T(1024)S(1)} %bitcast.53, f32[2048,128]{1,0:T(8,128)} %bitcast.47, f32[]{:T(128)} %constant.31.clone.1), kind=kCustom, calls=%fused_computation.27 | custom fusion | flops 262144 | bytes 2097664 | tf_op jit(solution)/shard_map/scatter-add | solution.py:111
  191.7 3.2 %multiply_subtract_fusion = f32[4096,128]{1,0:T(8,128)} fusion(f32[4096,128]{1,0:T(8,128)S(1)} %copy-done.2, f32[4096,128]{1,0:T(8,128)} %scatter_custom_fusion), kind=kLoop, calls=%fused_computation.22 | loop fusion | flops 1048576 | bytes 6291456 | tf_op jit(solution)/shard_map/sub | solution.py:113
  194.9 0.4 fusion.26
  195.4 4.6 %all_to_all.37 = f32[2,1024,128]{2,1,0:T(8,128)S(1)} all-to-all(f32[2,1024,128]{2,1,0:T(8,128)S(1)} %broadcast_in_dim.69), channel_id=1, replica_groups=mesh['dp'=64,'mp'=2] {'mp'}, dimensions={0} | all-to-all | bytes 2097152 | tf_op jit(solution)/shard_map/all_to_all | solution.py:17
  200.0 0.8 reduce_sum.28
  200.8 54.9 %all-reduce.3.cloned.1.call-done = (f32[1024,512]{1,0:T(8,128)}, f32[512,1024]{1,0:T(8,128)}, f32[1024,512]{1,0:T(8,128)}, f32[512,128]{1,0:T(8,128)}) async-done(((f32[1024,512]{1,0:T(8,128)}, f32[512,1024]{1,0:T(8,128)}, f32[1024,512]{1,0:T(8,128)}, f32[512,128]{1,0:T(8,128)}), (f32[1024,512]{1,0:T(8,128)}, f32[512,1024]{1,0:T(8,128)}, f32[1024,512]{1,0:T(8,128)}, ...) | async-done | bytes 6553616 | tf_op jit(solution)/shard_map/psum | solution.py:102
  255.7 3.2 %copy.49 = f32[1024,512]{1,0:T(8,128)} copy(f32[1024,512]{1,0:T(8,128)} %get-tuple-element.18) | data formatting | bytes 4194304
  259.0 1.3 copy.50
  260.3 1.0 copy-done.6
  261.3 1.3 copy.51
  262.6 0.7 copy.52
  (63 shorter events, 1.3 us)
Async XLA Ops:
  7.2 45.8 %copy-start = (bf16[1024,512]{1,0:T(8,128)(2,1)S(1)}, bf16[1024,512]{1,0:T(8,128)(2,1)}, u32[]{:S(2)}) copy-start(bf16[1024,512]{1,0:T(8,128)(2,1)} %param.21) | copy-start | bytes 3145732
  7.2 6.2 %copy-start.14 = (bf16[512,1024]{1,0:T(8,128)(2,1)S(1)}, bf16[512,1024]{1,0:T(8,128)(2,1)}, u32[]{:S(2)}) copy-start(bf16[512,1024]{1,0:T(8,128)(2,1)} %param.20) | copy-start | bytes 3145732
  7.2 35.8 %all-gather.5.cloned.1.call-start = ((), (), s32[]{:S(2)}) async-start(), calls=%async_computation.7 | async-start | bytes 12582912 | tf_op jit(solution)/shard_map/all_gather | solution.py:12
  12.0 1.3 copy-start.19
  16.6 66.1 %all-gather.7.cloned.1.call-start = ((), (), s32[]{:S(2)}) async-start(), calls=%async_computation.8 | async-start | bytes 12582912 | tf_op jit(solution)/shard_map/all_gather | solution.py:12
  53.0 1.6 copy-start.5
  53.0 1.6 copy-start.9
  53.0 1.6 copy-start.11
  54.5 4.4 %copy-start.3 = (bf16[1024,512]{1,0:T(8,128)(2,1)}, bf16[1024,512]{1,0:T(8,128)(2,1)S(1)}, u32[]{:S(2)}) copy-start(bf16[1024,512]{1,0:T(8,128)(2,1)S(1)} %get-tuple-element.13) | copy-start | bytes 3145732
  58.7 197.0 %all-reduce.3.cloned.1.call-start = ((), (), s32[]{:S(2)}) async-start(), calls=%async_computation.9 | async-start | bytes 13107200 | tf_op jit(solution)/shard_map/psum | solution.py:102
  89.4 5.1 %copy-start.20 = (f32[1024,512]{1,0:T(8,128)S(1)}, f32[1024,512]{1,0:T(8,128)}, u32[]{:S(2)}) copy-start(f32[1024,512]{1,0:T(8,128)} %copy-done.19) | copy-start | bytes 6291460
  94.5 2.7 copy-start.15
  94.5 2.7 copy-start.16
  94.5 2.7 copy-start.17
  94.5 2.7 copy-start.18
  105.3 0.7 copy-start.12
  105.3 27.2 %copy-start.2 = (f32[4096,128]{1,0:T(8,128)S(1)}, f32[4096,128]{1,0:T(8,128)}, u32[]{:S(2)}) copy-start(f32[4096,128]{1,0:T(8,128)} %param.15) | copy-start | bytes 6291460
  105.3 35.7 %copy-start.13 = (s32[1,64]{1,0:T(1,128)S(1)}, s32[1,64]{1,0:T(1,128)}, u32[]{:S(2)}) copy-start(s32[1,64]{1,0:T(1,128)} %param.13) | copy-start | bytes 772
  105.3 45.8 %copy-start.10 = (bf16[1,64,32,128]{3,2,1,0:T(8,128)(2,1)S(1)}, bf16[1,64,32,128]{3,2,1,0:T(8,128)(2,1)}, u32[]{:S(2)}) copy-start(bf16[1,64,32,128]{3,2,1,0:T(8,128)(2,1)} %param.14) | copy-start | bytes 1572868
  106.7 18.8 %all-to-all-start = ((s32[1,64,16]{2,0,1:T(1,128)}), s32[1,64,16]{2,0,1:T(1,128)S(1)}, u32[]{:S(2)}, u32[]{:S(2)}) async-start(s32[1,64,16]{2,0,1:T(1,128)} %copy.43), calls=%async_computation | async-start | bytes 65536 | tf_op jit(solution)/shard_map/all_to_all | solution.py:66
  126.3 10.1 %all-to-all-start.3 = ((s32[2,1,1024]{2,1,0:T(1,128)}), s32[2,1,1024]{2,1,0:T(1,128)S(1)}, u32[]{:S(2)}, u32[]{:S(2)}) async-start(s32[2,1,1024]{2,1,0:T(1,128)} %reshape.200), calls=%async_computation.3 | async-start | bytes 16384 | tf_op jit(solution)/shard_map/all_to_all | solution.py:17
  136.3 14.8 %all-to-all-start.1 = ((bf16[1,64,16,128]{3,2,0,1:T(8,128)(2,1)}), bf16[1,64,16,128]{3,2,0,1:T(8,128)(2,1)S(1)}, u32[]{:S(2)}, u32[]{:S(2)}) async-start(bf16[1,64,16,128]{3,2,0,1:T(8,128)(2,1)} %select_convert_fusion), calls=%async_computation.1 | async-start | bytes 524288 | tf_op jit(solution)/shard_map/all_to_all | solution.py:69
  157.3 14.7 %all-to-all-start.4 = ((bf16[1,64,16,128]{3,2,0,1:T(8,128)(2,1)}), bf16[1,64,16,128]{3,2,0,1:T(8,128)(2,1)S(1)}, u32[]{:S(2)}, u32[]{:S(2)}) async-start(bf16[1,64,16,128]{3,2,0,1:T(8,128)(2,1)} %get-tuple-element.11), calls=%async_computation.4 | async-start | bytes 524288 | tf_op jit(solution)/shard_map/all_to_all | solution.py:86
  191.7 3.2 %copy-start.4 = (bf16[1024,512]{1,0:T(8,128)(2,1)S(1)}, bf16[1024,512]{1,0:T(8,128)(2,1)}, u32[]{:S(2)}) copy-start(bf16[1024,512]{1,0:T(8,128)(2,1)} %copy-done.3) | copy-start | bytes 3145732
  255.7 3.2 %copy-start.7 = (f32[512,1024]{1,0:T(8,128)S(1)}, f32[512,1024]{1,0:T(8,128)}, u32[]{:S(2)}) copy-start(f32[512,1024]{1,0:T(8,128)} %get-tuple-element.19) | copy-start | bytes 6291460
  259.0 2.3 copy-start.6
  259.0 4.4 %copy-start.1 = (bf16[1024,512]{1,0:T(8,128)(2,1)S(1)}, bf16[1024,512]{1,0:T(8,128)(2,1)}, u32[]{:S(2)}) copy-start(bf16[1024,512]{1,0:T(8,128)(2,1)} %param.21) | copy-start | bytes 3145732
  261.3 1.3 copy-start.8
Sparse Core Ops, SparseCore 0:
  16.8 26.1 all-gather.4
  58.8 23.8 all-gather.6
  105.5 150.2 all-reduce.2
where the time goes:
time: 271 us; the launch traced here: 270 us
  waiting for transfers between devices  126 us (46%)
  other arithmetic  43.4 us (16%)
  matrix products  30.2 us (11%)
  starting transfers between devices  24.6 us (9%)
  local copies, waits for them, and re-layouts  16.5 us (6%)
  blocking collectives  15.1 us (6%)
  between operations  14.1 us (5%)
    psum x1, waiting for transfers between devices, local(): lax.psum((part_one, part_two, part_three, part_four), 'dp')  54.9 us
    all_gather x2, waiting for transfers between devices, over_pieces(): return lax.all_gather(array, axis).sum(0)  44.7 us
    all_to_all x3, blocking collectives, from_everyone(): lax.all_to_all(jnp.broadcast_to(array[None], (size, *array.shape)), axis,...  15.1 us
    reduce_sum x2, other arithmetic, over_pieces(): return lax.all_gather(array, axis).sum(0)  13.3 us
    scatter-add x1, other arithmetic, local(): delta = jnp.zeros_like(table).at[received.reshape(-1)].add(arrived.reshap...  13.2 us
    unnamed x50, local copies, waits for them, and re-layouts  11.2 us
    all_to_all x1, starting transfers between devices, local(): lax.all_to_all(mine, 'dp', split_axis=1, concat_axis=1, tiled=True)  10.1 us
    all_to_all x1, waiting for transfers between devices, local(): lax.all_to_all(own_cot, 'dp', split_axis=1, concat_axis=1, tiled=True)  9.19 us
  transfers between devices with their start and end apart: 7, of which 6 were waited for; matrix products, arithmetic and copies ran while one was open for 13% of the time, Pallas kernels for 0%

commit v1 on v0

--- a/solution.py
+++ b/solution.py
@@ -63,7 +63,11 @@
     span = slots_all // lax.axis_size("mp")
     begin = lax.axis_index("mp") * span
     mine = lax.dynamic_slice_in_dim(hot_rows, begin, span, 2)
-    received = lax.all_to_all(mine, "dp", split_axis=1, concat_axis=1, tiled=True)
+    y1 = lax.axis_size("dp")
+    response = jnp.split(mine, y1, 1)
+    b_now = jnp.stack(response, axis=0)
+    current_block = lax.all_to_all(b_now, "dp", 0, 0)
+    received = jnp.concatenate(current_block, 1)
     fetched = jnp.take(table, received.reshape(-1), axis=0).astype(jnp.bfloat16)
     fetched = fetched.reshape(received.shape + (width,))
     returned = lax.all_to_all(fetched, "dp", split_axis=1, concat_axis=1, tiled=True)

time: 271 us -> 274 us (1.011)
  local copies, waits for them, and re-layouts: 16.5 us -> 51.5 us
  waiting for transfers between devices: 126 us -> 94.9 us
    unnamed x50 -> x116, local copies, waits for them, and re-layouts: 11.2 us -> 43.6 us
    all_gather x2, waiting for transfers between devices: 44.7 us -> 15.4 us  [over_pieces(): return lax.all_gather(array, axis).sum(0)]
    psum x1, waiting for transfers between devices: 54.9 us -> 50.2 us  [local(): lax.psum((part_one, part_two, part_three, part_four), 'dp')]
  transfers between devices with their start and end apart: 7 -> 7, of which waited for: 6 -> 6; matrix products, arithmetic and copies ran while one was open for 13% -> 25% of each run, Pallas kernels for 0% -> 0%
where the time goes in v1:
time: 274 us; the launch traced here: 273 us
  waiting for transfers between devices  94.9 us (35%)
  local copies, waits for them, and re-layouts  51.5 us (19%)
  other arithmetic  43.4 us (16%)
  matrix products  30.3 us (11%)
  starting transfers between devices  24.6 us (9%)
  blocking collectives  14.6 us (5%)
  between operations  14.1 us (5%)
    psum x1, waiting for transfers between devices, local(): lax.psum((part_one, part_two, part_three, part_four), 'dp')  50.2 us
    unnamed x116, local copies, waits for them, and re-layouts  43.6 us
    all_gather x2, waiting for transfers between devices, over_pieces(): return lax.all_gather(array, axis).sum(0)  15.4 us
    all_to_all x3, blocking collectives, from_everyone(): lax.all_to_all(jnp.broadcast_to(array[None], (size, *array.shape)), axis,...  14.6 us
    reduce_sum x2, other arithmetic, over_pieces(): return lax.all_gather(array, axis).sum(0)  13.3 us
    scatter-add x1, other arithmetic, local(): delta = jnp.zeros_like(table).at[received.reshape(-1)].add(arrived.reshap...  13.2 us
    all_to_all x1, waiting for transfers between devices, local(): lax.all_to_all(fetched, 'dp', split_axis=1, concat_axis=1, tiled=True)  10.6 us
    all_to_all x1, starting transfers between devices, local(): current_block = lax.all_to_all(b_now, 'dp', 0, 0)  10.1 us
  transfers between devices with their start and end apart: 7, of which 6 were waited for; matrix products, arithmetic and copies ran while one was open for 25% of the time, Pallas kernels for 0%

profile of v1, /device:TPU:1, one launch (start us, length us, event | category | flops | bytes accessed | tf_op | source)
XLA Modules:
  0.0 273.3 jit_solution(14070160502204006496)
XLA Ops:
  7.2 4.8 %fusion.9 = f32[1024,512]{1,0:T(8,128)S(1)} fusion(bf16[1024,512]{1,0:T(8,128)(2,1)} %param.19, s32[1024]{0:T(1024)} %param.18, s32[1024]{0:T(1024)} %param.17, s32[1024]{0:T(1024)} %param.16), kind=kOutput, calls=%fused_computation.21 | convolution fusion | flops 1086324736 | bytes 3158016 | tf_op jit(solution)/shard_map/dot_general | solution.py:76
  12.0 1.3 copy-done.21
  13.4 3.3 %fusion.89 = f32[1024,1024]{1,0:T(8,128)} fusion(bf16[512,1024]{1,0:T(8,128)(2,1)S(1)} %copy-done.14, f32[1024,512]{1,0:T(8,128)S(1)} %fusion.9), kind=kOutput, calls=%fused_computation.241 | convolution fusion | flops 1076363264 | bytes 7340032 | tf_op jit(solution)/shard_map/dot_general | solution.py:78
  16.7 0.6 copy-done.2
  18.8 0.5 fusion.18
  19.3 0.5 constant_dynamic-update-slice_fusion.63
  28.0 15.0 %all-gather.5.cloned.1.call-done = f32[2048,1024]{1,0:T(8,128)} async-done(((f32[1024,1024]{1,0:T(8,128)}), f32[2048,1024]{1,0:T(8,128)}) %all-gather.5.cloned.1.call-update) | async-done | bytes 8388624 | tf_op jit(solution)/shard_map/all_gather | solution.py:12
  43.0 6.7 %reduce_sum.27 = f32[1024,1024]{1,0:T(8,128)} reduce(f32[2,1024,1024]{2,1,0:T(8,128)} %bitcast.170, f32[]{:T(128)} %constant.31.clone.1), dimensions={0}, to_apply=%region_1.2 | reduce | flops 1048576 | bytes 12582916 | tf_op jit(solution)/shard_map/reduce_sum | solution.py:12
  49.7 3.3 %multiply_convert_fusion.1 = bf16[1024,1024]{1,0:T(8,128)(2,1)S(1)} fusion(f32[1024,1024]{1,0:T(8,128)} %reduce_sum.27), kind=kLoop, calls=%fused_computation.8 | loop fusion | flops 5242880 | bytes 6291456 | tf_op jit(solution)/shard_map/convert_element_type | solution.py:79
  53.0 1.5 multiply_convert_fusion.4
  54.6 0.9 multiply_convert_fusion.3
  55.5 1.0 copy-done.19
  56.5 3.2 %fusion.91 = f32[1024,1024]{1,0:T(8,128)} fusion(bf16[1024,512]{1,0:T(8,128)(2,1)S(1)} %multiply_convert_fusion.3, bf16[1024,512]{1,0:T(8,128)(2,1)S(1)} %copy-done), kind=kOutput, calls=%fused_computation.245 | convolution fusion | flops 1073741824 | bytes 6291456 | tf_op jit(solution)/shard_map/dot_general | solution.py:97
  60.0 0.5 constant_dynamic-update-slice_fusion.46
  77.9 1.2 convolution_multiply_fusion.2
  79.1 4.2 %convolution_multiply_fusion = f32[1024,512]{1,0:T(8,128)} fusion(bf16[1024,1024]{1,0:T(8,128)(2,1)} %copy-done.6, bf16[1024,512]{1,0:T(8,128)(2,1)S(1)} %copy-done.20), kind=kOutput, calls=%fused_computation.23 | convolution fusion | flops 1074266112 | bytes 5242880 | tf_op jit(solution)/shard_map/dot_general | solution.py:99
  83.8 6.7 %reduce_sum.29 = f32[1024,1024]{1,0:T(8,128)} reduce(f32[2,1024,1024]{2,1,0:T(8,128)} %bitcast.171, f32[]{:T(128)} %constant.31.clone.1), dimensions={0}, to_apply=%region_3.4 | reduce | flops 1048576 | bytes 12582916 | tf_op jit(solution)/shard_map/reduce_sum | solution.py:12
  90.5 5.0 %multiply_convert_fusion = bf16[1024,1024]{1,0:T(8,128)(2,1)S(1)} fusion(f32[1024,1024]{1,0:T(8,128)} %reduce_sum.29, f32[1024,1024]{1,0:T(8,128)} %reduce_sum.27), kind=kLoop, calls=%fused_computation.7 | loop fusion | flops 9437184 | bytes 10485760 | tf_op jit(solution)/shard_map/convert_element_type | solution.py:100
  95.6 2.6 convolution_multiply_fusion.1
  98.2 8.1 %fusion.11 = f32[1024,512]{1,0:T(8,128)} fusion(s32[1024]{0:T(1024)S(1)} %copy-done.16, s32[1024]{0:T(1024)S(1)} %copy-done.17, s32[1024]{0:T(1024)S(1)} %copy-done.18, f32[1024,512]{1,0:T(8,128)} %copy-done.21, bf16[1024,1024]{1,0:T(8,128)(2,1)S(1)} %multiply_convert_fusion, bf16[512,1024]{1,0:T(8,128)(2,1)S(1)} %copy-done.15), kind=kOutput, calls=%fused_computation.25 | convolution fusion | flops 2165309440 | bytes 7352320 | tf_op jit(solution)/shard_map/dot_general | solution.py:105
  112.5 10.1 %all-to-all-start = ((s32[64,1,1,16]{3,2,1,0:T(1,128)}), s32[64,1,1,16]{3,2,1,0:T(1,128)S(1)}, u32[]{:S(2)}, u32[]{:S(2)}) async-start(s32[64,1,1,16]{3,2,1,0:T(1,128)} %constant_dynamic-update-slice_fusion), calls=%async_computation | async-start | bytes 65536 | tf_op jit(solution)/shard_map/all_to_all | solution.py:69
  122.7 8.7 %all-to-all-done = s32[64,1,1,16]{3,2,1,0:T(1,128)S(1)} async-done(((s32[64,1,1,16]{3,2,1,0:T(1,128)}), s32[64,1,1,16]{3,2,1,0:T(1,128)S(1)}, u32[]{:S(2)}, u32[]{:S(2)}) %all-to-all-start) | async-done | bytes 4128 | tf_op jit(solution)/shard_map/all_to_all | solution.py:69
  131.4 0.7 reshape.257
  132.1 4.8 %all-to-all-start.3 = ((s32[2,1,1024]{2,1,0:T(1,128)}), s32[2,1,1024]{2,1,0:T(1,128)S(1)}, u32[]{:S(2)}, u32[]{:S(2)}) async-start(s32[2,1,1024]{2,1,0:T(1,128)} %reshape.257), calls=%async_computation.3 | async-start | bytes 16384 | tf_op jit(solution)/shard_map/all_to_all | solution.py:17
  137.5 0.7 reduce.131
  138.3 2.9 %gather_fusion = bf16[1024,128]{1,0:T(8,128)(2,1)S(1)} fusion(f32[4096,128]{1,0:T(8,128)S(1)} %copy-done.3, s32[1024]{0:T(1024)S(1)} %broadcast_clamp_fusion), kind=kCustom, calls=%fused_computation | custom fusion | bytes 528384 | tf_op jit(solution)/shard_map/jit(_take)/gather | solution.py:71
  141.2 0.9 select_convert_fusion
  142.2 4.7 %all-to-all-start.1 = ((bf16[1,64,16,128]{3,2,0,1:T(8,128)(2,1)}), bf16[1,64,16,128]{3,2,0,1:T(8,128)(2,1)S(1)}, u32[]{:S(2)}, u32[]{:S(2)}) async-start(bf16[1,64,16,128]{3,2,0,1:T(8,128)(2,1)} %select_convert_fusion), calls=%async_computation.1 | async-start | bytes 524288 | tf_op jit(solution)/shard_map/all_to_all | solution.py:73
  146.9 0.5 broadcast.204
  147.4 0.7 reduce.132
  148.4 10.6 %all-to-all-done.1 = bf16[1,64,16,128]{3,2,0,1:T(8,128)(2,1)S(1)} async-done(((bf16[1,64,16,128]{3,2,0,1:T(8,128)(2,1)}), bf16[1,64,16,128]{3,2,0,1:T(8,128)(2,1)S(1)}, u32[]{:S(2)}, u32[]{:S(2)}) %all-to-all-start.1) | async-done | bytes 262176 | tf_op jit(solution)/shard_map/all_to_all | solution.py:73
  159.1 0.9 dynamic-slice_select_fusion
  160.0 4.9 %all_to_all.35 = bf16[2,1,64,16,128]{4,3,2,1,0:T(8,128)(2,1)S(1)} all-to-all(bf16[2,1,64,16,128]{4,3,2,1,0:T(8,128)(2,1)S(1)} %broadcast_in_dim.63), channel_id=1, replica_groups=mesh['dp'=64,'mp'=2] {'mp'}, dimensions={0} | all-to-all | bytes 1048576 | tf_op jit(solution)/shard_map/all_to_all | solution.py:17
  164.9 4.7 %all-to-all-start.4 = ((bf16[1,64,16,128]{3,2,0,1:T(8,128)(2,1)}), bf16[1,64,16,128]{3,2,0,1:T(8,128)(2,1)S(1)}, u32[]{:S(2)}, u32[]{:S(2)}) async-start(bf16[1,64,16,128]{3,2,0,1:T(8,128)(2,1)} %get-tuple-element.75), calls=%async_computation.4 | async-start | bytes 524288 | tf_op jit(solution)/shard_map/all_to_all | solution.py:90
  169.6 0.8 copy.231
  170.4 9.8 %all-to-all-done.4 = bf16[1,64,16,128]{3,2,0,1:T(8,128)(2,1)S(1)} async-done(((bf16[1,64,16,128]{3,2,0,1:T(8,128)(2,1)}), bf16[1,64,16,128]{3,2,0,1:T(8,128)(2,1)S(1)}, u32[]{:S(2)}, u32[]{:S(2)}) %all-to-all-start.4) | async-done | bytes 262176 | tf_op jit(solution)/shard_map/all_to_all | solution.py:90
  180.3 5.2 %all_to_all.36 = bf16[2,1,64,16,128]{4,3,2,1,0:T(8,128)(2,1)S(1)} all-to-all(bf16[2,1,64,16,128]{4,3,2,1,0:T(8,128)(2,1)S(1)} %broadcast_in_dim.67), channel_id=1, replica_groups=mesh['dp'=64,'mp'=2] {'mp'}, dimensions={0} | all-to-all | bytes 1048576 | tf_op jit(solution)/shard_map/all_to_all | solution.py:17
  185.5 1.1 copy_convert_fusion
  186.6 13.2 %scatter_custom_fusion = f32[4096,128]{1,0:T(8,128)} fusion(s32[2048]{0:T(1024)S(1)} %bitcast.180, f32[2048,128]{1,0:T(8,128)} %bitcast.174, f32[]{:T(128)} %constant.31.clone.1), kind=kCustom, calls=%fused_computation.27 | custom fusion | flops 262144 | bytes 2097664 | tf_op jit(solution)/shard_map/scatter-add | solution.py:115
  199.8 3.2 %multiply_subtract_fusion = f32[4096,128]{1,0:T(8,128)} fusion(f32[4096,128]{1,0:T(8,128)S(1)} %copy-done.3, f32[4096,128]{1,0:T(8,128)} %scatter_custom_fusion), kind=kLoop, calls=%fused_computation.22 | loop fusion | flops 1048576 | bytes 6291456 | tf_op jit(solution)/shard_map/sub | solution.py:117
  203.6 4.6 %all_to_all.37 = f32[2,1024,128]{2,1,0:T(8,128)S(1)} all-to-all(f32[2,1024,128]{2,1,0:T(8,128)S(1)} %broadcast_in_dim.68), channel_id=1, replica_groups=mesh['dp'=64,'mp'=2] {'mp'}, dimensions={0} | all-to-all | bytes 2097152 | tf_op jit(solution)/shard_map/all_to_all | solution.py:17
  208.1 0.8 reduce_sum.28
  208.9 50.2 %all-reduce.3.cloned.1.call-done = (f32[1024,512]{1,0:T(8,128)}, f32[512,1024]{1,0:T(8,128)}, f32[1024,512]{1,0:T(8,128)}, f32[512,128]{1,0:T(8,128)}) async-done(((f32[1024,512]{1,0:T(8,128)}, f32[512,1024]{1,0:T(8,128)}, f32[1024,512]{1,0:T(8,128)}, f32[512,128]{1,0:T(8,128)}), (f32[1024,512]{1,0:T(8,128)}, f32[512,1024]{1,0:T(8,128)}, f32[1024,512]{1,0:T(8,128)}, ...) | async-done | bytes 6553616 | tf_op jit(solution)/shard_map/psum | solution.py:106
  259.2 3.2 %copy.304 = f32[1024,512]{1,0:T(8,128)} copy(f32[1024,512]{1,0:T(8,128)} %get-tuple-element.82) | data formatting | bytes 4194304
  262.4 1.3 copy.305
  263.8 1.0 copy-done.7
  264.8 1.3 copy.306
  266.1 0.7 copy.307
  (133 shorter events, 35.8 us)
Async XLA Ops:
  7.2 45.8 %copy-start = (bf16[1024,512]{1,0:T(8,128)(2,1)S(1)}, bf16[1024,512]{1,0:T(8,128)(2,1)}, u32[]{:S(2)}) copy-start(bf16[1024,512]{1,0:T(8,128)(2,1)} %param.21) | copy-start | bytes 3145732
  7.2 6.2 %copy-start.14 = (bf16[512,1024]{1,0:T(8,128)(2,1)S(1)}, bf16[512,1024]{1,0:T(8,128)(2,1)}, u32[]{:S(2)}) copy-start(bf16[512,1024]{1,0:T(8,128)(2,1)} %param.20) | copy-start | bytes 3145732
  7.2 35.8 %all-gather.5.cloned.1.call-start = ((), (), s32[]{:S(2)}) async-start(), calls=%async_computation.7 | async-start | bytes 12582912 | tf_op jit(solution)/shard_map/all_gather | solution.py:12
  12.0 1.3 copy-start.21
  16.6 0.7 copy-start.2
  16.6 67.2 %all-gather.7.cloned.1.call-start = ((), (), s32[]{:S(2)}) async-start(), calls=%async_computation.8 | async-start | bytes 12582912 | tf_op jit(solution)/shard_map/all_gather | solution.py:12
  53.0 1.6 copy-start.6
  53.0 1.6 copy-start.10
  53.0 1.6 copy-start.12
  54.6 23.3 %copy-start.4 = (bf16[1024,512]{1,0:T(8,128)(2,1)}, bf16[1024,512]{1,0:T(8,128)(2,1)S(1)}, u32[]{:S(2)}) copy-start(bf16[1024,512]{1,0:T(8,128)(2,1)S(1)} %get-tuple-element.77) | copy-start | bytes 3145732
  55.5 1.0 copy-start.19
  59.7 19.4 %copy-start.20 = (bf16[1024,512]{1,0:T(8,128)(2,1)S(1)}, bf16[1024,512]{1,0:T(8,128)(2,1)}, u32[]{:S(2)}) copy-start(bf16[1024,512]{1,0:T(8,128)(2,1)} %copy-done.19) | copy-start | bytes 3145732
  59.7 199.5 %all-reduce.3.cloned.1.call-start = ((), (), s32[]{:S(2)}) async-start(), calls=%async_computation.9 | async-start | bytes 13107200 | tf_op jit(solution)/shard_map/psum | solution.py:106
  90.5 5.1 %copy-start.22 = (f32[1024,512]{1,0:T(8,128)S(1)}, f32[1024,512]{1,0:T(8,128)}, u32[]{:S(2)}) copy-start(f32[1024,512]{1,0:T(8,128)} %copy-done.21) | copy-start | bytes 6291460
  95.5 2.7 copy-start.15
  95.5 2.7 copy-start.16
  95.6 2.7 copy-start.17
  95.6 2.7 copy-start.18
  106.3 32.0 %copy-start.3 = (f32[4096,128]{1,0:T(8,128)S(1)}, f32[4096,128]{1,0:T(8,128)}, u32[]{:S(2)}) copy-start(f32[4096,128]{1,0:T(8,128)} %param.15) | copy-start | bytes 6291460
  106.4 40.4 %copy-start.13 = (s32[1,64]{1,0:T(1,128)S(1)}, s32[1,64]{1,0:T(1,128)}, u32[]{:S(2)}) copy-start(s32[1,64]{1,0:T(1,128)} %param.13) | copy-start | bytes 772
  106.4 52.7 %copy-start.11 = (bf16[1,64,32,128]{3,2,1,0:T(8,128)(2,1)S(1)}, bf16[1,64,32,128]{3,2,1,0:T(8,128)(2,1)}, u32[]{:S(2)}) copy-start(bf16[1,64,32,128]{3,2,1,0:T(8,128)(2,1)} %param.14) | copy-start | bytes 1572868
  112.5 18.8 %all-to-all-start = ((s32[64,1,1,16]{3,2,1,0:T(1,128)}), s32[64,1,1,16]{3,2,1,0:T(1,128)S(1)}, u32[]{:S(2)}, u32[]{:S(2)}) async-start(s32[64,1,1,16]{3,2,1,0:T(1,128)} %constant_dynamic-update-slice_fusion), calls=%async_computation | async-start | bytes 65536 | tf_op jit(solution)/shard_map/all_to_all | solution.py:69
  132.1 10.0 %all-to-all-start.3 = ((s32[2,1,1024]{2,1,0:T(1,128)}), s32[2,1,1024]{2,1,0:T(1,128)S(1)}, u32[]{:S(2)}, u32[]{:S(2)}) async-start(s32[2,1,1024]{2,1,0:T(1,128)} %reshape.257), calls=%async_computation.3 | async-start | bytes 16384 | tf_op jit(solution)/shard_map/all_to_all | solution.py:17
  142.2 16.9 %all-to-all-start.1 = ((bf16[1,64,16,128]{3,2,0,1:T(8,128)(2,1)}), bf16[1,64,16,128]{3,2,0,1:T(8,128)(2,1)S(1)}, u32[]{:S(2)}, u32[]{:S(2)}) async-start(bf16[1,64,16,128]{3,2,0,1:T(8,128)(2,1)} %select_convert_fusion), calls=%async_computation.1 | async-start | bytes 524288 | tf_op jit(solution)/shard_map/all_to_all | solution.py:73
  164.9 15.4 %all-to-all-start.4 = ((bf16[1,64,16,128]{3,2,0,1:T(8,128)(2,1)}), bf16[1,64,16,128]{3,2,0,1:T(8,128)(2,1)S(1)}, u32[]{:S(2)}, u32[]{:S(2)}) async-start(bf16[1,64,16,128]{3,2,0,1:T(8,128)(2,1)} %get-tuple-element.75), calls=%async_computation.4 | async-start | bytes 524288 | tf_op jit(solution)/shard_map/all_to_all | solution.py:90
  199.8 3.2 %copy-start.5 = (bf16[1024,512]{1,0:T(8,128)(2,1)S(1)}, bf16[1024,512]{1,0:T(8,128)(2,1)}, u32[]{:S(2)}) copy-start(bf16[1024,512]{1,0:T(8,128)(2,1)} %copy-done.4) | copy-start | bytes 3145732
  259.2 3.2 %copy-start.8 = (f32[512,1024]{1,0:T(8,128)S(1)}, f32[512,1024]{1,0:T(8,128)}, u32[]{:S(2)}) copy-start(f32[512,1024]{1,0:T(8,128)} %get-tuple-element.83) | copy-start | bytes 6291460
  262.4 2.3 copy-start.7
  262.4 4.4 %copy-start.1 = (bf16[1024,512]{1,0:T(8,128)(2,1)S(1)}, bf16[1024,512]{1,0:T(8,128)(2,1)}, u32[]{:S(2)}) copy-start(bf16[1024,512]{1,0:T(8,128)(2,1)} %param.21) | copy-start | bytes 3145732
  264.8 1.3 copy-start.9
Sparse Core Ops, SparseCore 0:
  16.8 26.1 all-gather.4
  59.9 23.8 all-gather.6
  106.5 152.6 all-reduce.2
